TPU v7x, 32 devices: a whole 2x2x4 slice. The times are simulated.
32 devices in a mesh: slab: 4 (over x, core), rep: 8 (over z, y).
Axes of the slice: x: 2, y: 2, z: 4, core: 2. Of those that a mesh axis runs over, the one named last changes fastest.
Arguments:
- image: float32 [144, 256, 256], P('slab', 'rep'), may hold values from 0.5 to 2
- sensitivity: float32 [144, 256, 256], P('slab', 'rep'), may hold values from 0.5 to 2
- system_blocks: bfloat16 [512, 128, 1024], P(('slab', 'rep')), may hold values from 0 to 0.00390625
- tile_slab: int32 [512, 1], P(('slab', 'rep')), may hold values from 0 to 3; in each aligned block of 16 rows (0 to 15, 16 to 31, ...) at most 6 rows name the same one
- tile_block: int32 [512], P(('slab', 'rep')), may hold values from 0 to 2303
- background: bfloat16 [512, 128], P(('slab', 'rep')), may hold values from 0.19921875 to 1
Outputs:
- updated: float32 [144, 256, 256], P('slab', 'rep')
Inputs may be any that keep to these rules, and one draw needn't show every extreme that they name: `tile_slab`: among the 16 tiles of one device at most 6 view the same slab, and in some devices some slab is viewed by exactly 6.
All inputs are finite; a program needn't handle non-finite values.
Results may differ from a plain program's by a relative error of at most 0.0003.
Values may be sent and summed in bfloat16 or wider, within the bound.
No kernel may reach another device: no remote copies, remote signals or barrier semaphores. Data moves between devices by JAX's collectives and lax.ppermute only.
A program may use at most 64 MiB of HBM per device.

v0:
```python
import jax
import jax.numpy as jnp
from jax import lax
from jax.sharding import PartitionSpec as P

CAP = 6


def local(image, sensitivity, system_blocks, tile_slab, tile_block, background):
    slab_count = lax.axis_size("slab")
    tiles_here, tile_rows, width = system_blocks.shape
    destination = tile_slab[:, 0]
    replica_total = lax.axis_size("rep")
    detector_plane_count, local_rows, column_count = image.shape
    local_blocks = image.astype(jnp.bfloat16).reshape(-1, width)
    per_plane = local_rows * replica_total * column_count // width
    per_owner = local_rows * column_count // width
    within = tile_block % per_plane
    plane_of = tile_block // per_plane
    owner_rep = within // per_owner
    local_id = plane_of * per_owner + within % per_owner
    key = destination * replica_total + owner_rep
    key_hot = (
        key[:, None] == jnp.arange(slab_count * replica_total, dtype=jnp.int32)[None, :]
    ).astype(jnp.int32)
    position_order = jnp.sum((jnp.cumsum(key_hot, axis=0) - key_hot) * key_hot, axis=1)
    id_buffer = (
        jnp.zeros((slab_count, replica_total, CAP), jnp.int32)
        .at[destination, owner_rep, position_order]
        .set(local_id)
    )
    asked = lax.all_to_all(
        lax.all_to_all(id_buffer, "slab", split_axis=0, concat_axis=0, tiled=True),
        "rep",
        split_axis=1,
        concat_axis=1,
        tiled=True,
    )
    served_requests = local_blocks[asked]
    returned = lax.all_to_all(
        lax.all_to_all(served_requests, "slab", split_axis=0, concat_axis=0, tiled=True),
        "rep",
        split_axis=1,
        concat_axis=1,
        tiled=True,
    )
    emission_cell_entries = returned[destination, owner_rep, position_order]
    forward_projection = jnp.einsum(
        "tev,tv->te", system_blocks, emission_cell_entries, preferred_element_type=jnp.float32
    )
    inverse_permutation = (1.0 / (forward_projection + background.astype(jnp.float32))).astype(
        jnp.bfloat16
    )
    own_back = jnp.einsum(
        "tev,te->tv", system_blocks, inverse_permutation, preferred_element_type=jnp.float32
    )
    back_buffer = (
        jnp.zeros((slab_count, replica_total, CAP, width), jnp.float32)
        .at[destination, owner_rep, position_order]
        .set(own_back)
    )
    received_tiles = lax.all_to_all(
        lax.all_to_all(back_buffer, "slab", split_axis=0, concat_axis=0, tiled=True),
        "rep",
        split_axis=1,
        concat_axis=1,
        tiled=True,
    )
    owned = (
        jnp.zeros(local_blocks.shape, jnp.float32)
        .at[asked.reshape(-1)]
        .add(received_tiles.reshape(-1, width))
    )
    return image * owned.reshape(image.shape) / sensitivity


def solution(mesh):
    return jax.shard_map(
        local,
        mesh=mesh,
        in_specs=(
            P("slab", "rep", None),
            P("slab", "rep", None),
            P(("slab", "rep"), None, None),
            P(("slab", "rep"), None),
            P(("slab", "rep")),
            P(("slab", "rep"), None),
        ),
        out_specs=P("slab", "rep", None),
        check_vma=False,
    )
```

profile of v0, /device:TPU:0, one launch (start us, length us, event | category | flops | bytes accessed | tf_op | source)
XLA Modules:
  0.0 104.5 jit_solution(2315465785091688998)
XLA Ops:
  0.0 0.0 copy-start.1
  0.0 0.8 fusion.8
  0.8 0.7 bitcast_add_fusion
  1.4 0.1 fusion.6
  1.6 0.2 select_reduce_fusion
  1.7 0.7 fusion.12
  2.4 1.5 %scatter_fusion = s32[4,8,6]{1,0,2:T(4,128)S(1)} fusion(s32[4,8,6]{1,0,2:T(4,128)S(1)} %broadcast.74, s32[16]{0:T(128)S(1)} %get-tuple-element.8, s32[16]{0:T(128)S(1)} %get-tuple-element.5), kind=kCustom, calls=%fused_computation.2 | custom fusion | bytes 384 | tf_op jit(solution)/shard_map/scatter | solution.py:30
  3.9 7.9 %all_to_all.30 = s32[4,8,6]{1,2,0:T(8,128)S(1)} all-to-all(s32[4,8,6]{1,2,0:T(8,128)S(1)} %copy.23), channel_id=1, replica_groups=mesh['slab'=4,'rep'=8] {'slab'}, dimensions={0} | all-to-all | bytes 1536 | tf_op jit(solution)/shard_map/all_to_all | solution.py:33
  11.8 0.7 copy.24
  12.5 5.8 %all-to-all-start.1 = ((s32[4,8,6]{2,0,1:T(4,128)}), s32[4,8,6]{2,0,1:T(4,128)S(1)}, u32[]{:S(2)}, u32[]{:S(2)}) async-start(s32[4,8,6]{2,0,1:T(4,128)} %copy.24), calls=%async_computation.1 | async-start | bytes 32768 | tf_op jit(solution)/shard_map/all_to_all | solution.py:32
  18.4 0.0 copy-done.1
  18.4 0.1 convert_element_type.13
  18.5 0.4 reshape.57
  18.8 6.1 %all-to-all-done.1 = s32[4,8,6]{2,0,1:T(4,128)S(1)} async-done(((s32[4,8,6]{2,0,1:T(4,128)}), s32[4,8,6]{2,0,1:T(4,128)S(1)}, u32[]{:S(2)}, u32[]{:S(2)}) %all-to-all-start.1) | async-done | bytes 800 | tf_op jit(solution)/shard_map/all_to_all | solution.py:32
  24.9 0.1 copy.26
  25.1 0.1 copy.29
  25.2 0.1 reshape.62
  25.3 1.0 gather_fusion
  26.3 0.1 reshape.61
  26.4 0.2 copy.30
  26.7 9.8 %all_to_all.31 = bf16[4,8,6,1024]{3,1,2,0:T(8,128)(2,1)S(1)} all-to-all(bf16[4,8,6,1024]{3,1,2,0:T(8,128)(2,1)S(1)} %copy.30), channel_id=1, replica_groups=mesh['slab'=4,'rep'=8] {'slab'}, dimensions={0} | all-to-all | bytes 786432 | tf_op jit(solution)/shard_map/all_to_all | solution.py:41
  36.5 0.3 copy.31
  36.8 14.4 %all_to_all.32 = bf16[4,8,6,1024]{3,0,2,1:T(4,128)(2,1)S(1)} all-to-all(bf16[4,8,6,1024]{3,0,2,1:T(4,128)(2,1)S(1)} %copy.31), channel_id=1, replica_groups=mesh['slab'=4,'rep'=8] {'rep'}, dimensions={1} | all-to-all | bytes 786432 | tf_op jit(solution)/shard_map/all_to_all | solution.py:40
  51.2 0.2 copy.32
  51.4 0.7 gather_fusion.1
  52.1 0.0 copy-start.2
  52.1 0.0 copy-start
  52.1 3.5 %fusion.2 = f32[16,1,128]{2,1,0:T(1,128)S(1)} fusion(bf16[16,128,1024]{2,1,0:T(8,128)(2,1)} %param.8, bf16[16,1024,1]{1,0,2:T(8,128)(2,1)S(1)} %bitcast.32), kind=kOutput, calls=%fused_computation.9 | convolution fusion | flops 4194304 | bytes 4235264 | tf_op jit(solution)/shard_map/tev,tv->te/dot_general | solution.py:48
  55.6 0.0 copy-done.2
  55.7 0.0 copy-done
  55.7 0.7 fusion.4
  56.4 0.1 broadcast_in_dim.10
  56.4 1.6 %scatter_fusion.1 = f32[4,8,6,1024]{3,1,2,0:T(8,128)S(1)} fusion(f32[4,8,6,1024]{3,1,2,0:T(8,128)S(1)} %broadcast_in_dim.10, s32[16]{0:T(128)S(1)} %get-tuple-element.8, f32[16,1024]{1,0:T(8,128)S(1)} %bitcast.33), kind=kCustom, calls=%fused_computation.3 | custom fusion | bytes 196800 | tf_op jit(solution)/shard_map/scatter | solution.py:60
  58.0 14.0 %all_to_all.33 = f32[4,8,6,1024]{3,1,2,0:T(8,128)S(1)} all-to-all(f32[4,8,6,1024]{3,1,2,0:T(8,128)S(1)} %scatter_fusion.1), channel_id=1, replica_groups=mesh['slab'=4,'rep'=8] {'slab'}, dimensions={0} | all-to-all | bytes 1572864 | tf_op jit(solution)/shard_map/all_to_all | solution.py:63
  72.1 1.4 %copy.33 = f32[4,8,6,1024]{3,0,2,1:T(4,128)} copy(f32[4,8,6,1024]{3,1,2,0:T(8,128)S(1)} %all_to_all.33) | data formatting | bytes 1572864 | tf_op jit(solution)/shard_map/all_to_all | solution.py:63
  73.5 3.5 %all-to-all-start.5 = ((f32[4,8,6,1024]{3,0,2,1:T(4,128)}), f32[4,8,6,1024]{3,0,2,1:T(4,128)S(1)}, u32[]{:S(2)}, u32[]{:S(2)}) async-start(f32[4,8,6,1024]{3,0,2,1:T(4,128)} %copy.33), calls=%async_computation.5 | async-start | bytes 1572864 | tf_op jit(solution)/shard_map/all_to_all | solution.py:62
  77.0 0.1 reshape.56
  77.2 19.9 %all-to-all-done.5 = f32[4,8,6,1024]{3,0,2,1:T(4,128)S(1)} async-done(((f32[4,8,6,1024]{3,0,2,1:T(4,128)}), f32[4,8,6,1024]{3,0,2,1:T(4,128)S(1)}, u32[]{:S(2)}, u32[]{:S(2)}) %all-to-all-start.5) | async-done | bytes 786464 | tf_op jit(solution)/shard_map/all_to_all | solution.py:62
  97.1 0.5 copy.34
  97.6 1.0 reshape.90
  98.6 3.0 %scatter_custom_fusion.2 = f32[288,1024]{1,0:T(8,128)S(1)} fusion(s32[192]{0:T(256)S(1)} %bitcast.36, f32[192,1024]{1,0:T(8,128)} %reshape.90, f32[]{:T(128)} %constant.55.clone.1), kind=kCustom, calls=%fused_computation.6 | custom fusion | flops 196608 | bytes 1180160 | tf_op jit(solution)/shard_map/scatter-add | solution.py:72
  101.6 0.3 reshape.59
  101.9 2.6 %multiply_divide_fusion = f32[36,32,256]{2,1,0:T(8,128)} fusion(f32[36,32,256]{2,1,0:T(8,128)} %param.7, f32[36,32,256]{2,1,0:T(8,128)S(1)} %copy-done.1, f32[36,32,256]{2,1,0:T(8,128)S(1)} %reshape.59), kind=kLoop, calls=%fused_computation.5 | loop fusion | flops 589824 | bytes 4718592 | tf_op jit(solution)/shard_map/div | solution.py:74
  (9 shorter events, 0.1 us)
Async XLA Ops:
  0.0 18.4 %copy-start.1 = (f32[36,32,256]{2,1,0:T(8,128)S(1)}, f32[36,32,256]{2,1,0:T(8,128)}, u32[]{:S(2)}) copy-start(f32[36,32,256]{2,1,0:T(8,128)} %param.6) | copy-start | bytes 3538948
  12.5 12.4 %all-to-all-start.1 = ((s32[4,8,6]{2,0,1:T(4,128)}), s32[4,8,6]{2,0,1:T(4,128)S(1)}, u32[]{:S(2)}, u32[]{:S(2)}) async-start(s32[4,8,6]{2,0,1:T(4,128)} %copy.24), calls=%async_computation.1 | async-start | bytes 32768 | tf_op jit(solution)/shard_map/all_to_all | solution.py:32
  52.1 3.5 %copy-start.2 = (bf16[16,128]{1,0:T(8,128)(2,1)S(1)}, bf16[16,128]{1,0:T(8,128)(2,1)}, u32[]{:S(2)}) copy-start(bf16[16,128]{1,0:T(8,128)(2,1)} %param.11) | copy-start | bytes 12292
  52.1 3.6 %copy-start = (bf16[16,128,1024]{2,1,0:T(8,128)(2,1)S(1)}, bf16[16,128,1024]{2,1,0:T(8,128)(2,1)}, u32[]{:S(2)}) copy-start(bf16[16,128,1024]{2,1,0:T(8,128)(2,1)} %param.8) | copy-start | bytes 12582916
  73.5 23.6 %all-to-all-start.5 = ((f32[4,8,6,1024]{3,0,2,1:T(4,128)}), f32[4,8,6,1024]{3,0,2,1:T(4,128)S(1)}, u32[]{:S(2)}, u32[]{:S(2)}) async-start(f32[4,8,6,1024]{3,0,2,1:T(4,128)} %copy.33), calls=%async_computation.5 | async-start | bytes 1572864 | tf_op jit(solution)/shard_map/all_to_all | solution.py:62
where the time goes:
time: 105 us
  blocking collectives  46.1 us (44%)
  waiting for transfers between devices  26.1 us (25%)
  local copies, waits for them, and re-layouts  10.5 us (10%)
  starting transfers between devices  9.38 us (9%)
  other arithmetic  8.13 us (8%)
  matrix products  4.17 us (4%)
    all_to_all x1, waiting for transfers between devices, local(): lax.all_to_all(lax.all_to_all(back_buffer, 'slab', split_axis=0, concat_a...  19.9 us
    all_to_all x1, blocking collectives, local(): lax.all_to_all(lax.all_to_all(served_requests, 'slab', split_axis=0, conc...  14.4 us
    all_to_all x1, blocking collectives, local(): lax.all_to_all(back_buffer, 'slab', split_axis=0, concat_axis=0, tiled=True)  14 us
    all_to_all x1, blocking collectives, local(): lax.all_to_all(served_requests, 'slab', split_axis=0, concat_axis=0, tile...  9.8 us
    all_to_all x1, blocking collectives, local(): lax.all_to_all(id_buffer, 'slab', split_axis=0, concat_axis=0, tiled=True)  7.9 us
    all_to_all x1, waiting for transfers between devices, local(): lax.all_to_all(lax.all_to_all(id_buffer, 'slab', split_axis=0, concat_axi...  6.12 us
    all_to_all x1, starting transfers between devices, local(): lax.all_to_all(lax.all_to_all(id_buffer, 'slab', split_axis=0, concat_axi...  5.83 us
    all_to_all x1, starting transfers between devices, local(): lax.all_to_all(lax.all_to_all(back_buffer, 'slab', split_axis=0, concat_a...  3.55 us
  transfers between devices with their start and end apart: 2, of which 2 were waited for; matrix products, arithmetic and copies ran while one was open for 1% of the time, Pallas kernels for 0%

commit v1 on v0

v1 whole, which is shorter than its diff:
```python
import functools
import jax
import jax.numpy as jnp
from jax import lax
from jax.experimental import pallas as pl
from jax.experimental.pallas import tpu as pltpu
from jax.sharding import PartitionSpec as P

CAP = 6
LANES = 128
SUB = 8
AXES = ("slab", "rep")
SMEM = pltpu.SMEM
VMEM = pltpu.VMEM


def spec(space):
    return pl.BlockSpec(memory_space=space)


def half_rows():
    return lax.broadcasted_iota(jnp.int32, (SUB, LANES), 0) < SUB // 2


def route_kernel(slab_ref, block_ref, ids_ref, slot_ref, *, peers, reps, per_plane, per_owner, cap):
    for d in range(peers):
        ids_ref[d * LANES] = 0
    for t in range(slot_ref.shape[0]):
        block = block_ref[t]
        plane = lax.div(block, per_plane)
        within = lax.rem(block, per_plane)
        d = slab_ref[t] * reps + lax.div(within, per_owner)
        position = ids_ref[d * LANES]
        ids_ref[d * LANES] = position + 1
        ids_ref[d * LANES + 1 + position] = plane * per_owner + lax.rem(within, per_owner)
        slot_ref[t] = d * cap + position


def serve_kernel(ids_ref, image_ref, out_ref, *, peers, cap):
    top = half_rows()

    def peer(d, carry):
        def row(j, inner):
            local_id = ids_ref[d * LANES + 1 + j]
            tile = image_ref[lax.div(local_id, 2)]
            left, right = tile[:, :LANES], tile[:, LANES:]
            even = jnp.where(top, left, pltpu.roll(right, SUB // 2, 0))
            odd = jnp.where(top, pltpu.roll(left, SUB // 2, 0), right)
            picked = jnp.where(lax.rem(local_id, 2) == 0, even, odd)
            out_ref[d * cap + j] = picked.astype(jnp.bfloat16)
            return inner

        return lax.fori_loop(0, ids_ref[d * LANES], row, carry)

    lax.fori_loop(0, peers, peer, 0)


def project_kernel(slot_ref, blocks_ref, system_ref, background_ref, out_ref):
    half = SUB // 2
    order = [(k % 2) * half + k // 2 for k in range(SUB)]
    for t in range(system_ref.shape[0]):
        slot = slot_ref[t]
        block = blocks_ref[slot].astype(jnp.float32)
        line = jnp.concatenate([block[j : j + 1] for j in order], axis=1).astype(jnp.bfloat16)
        system = system_ref[t]
        forward = lax.dot_general(
            line, system, (((1,), (1,)), ((), ())), preferred_element_type=jnp.float32
        )
        inverse = (1.0 / (forward + background_ref[t : t + 1].astype(jnp.float32))).astype(
            jnp.bfloat16
        )
        back = jnp.dot(inverse, system, preferred_element_type=jnp.float32)
        out_ref[slot] = jnp.concatenate(
            [back[:, order.index(j) * LANES : (order.index(j) + 1) * LANES] for j in range(SUB)],
            axis=0,
        )


def update_kernel(ids_ref, back_ref, image_ref, sensitivity_ref, out_ref, *, peers, cap):
    top = half_rows()
    out_ref[...] = jnp.zeros(out_ref.shape, jnp.float32)

    def peer(d, carry):
        def row(j, inner):
            local_id = ids_ref[d * LANES + 1 + j]
            group = lax.div(local_id, 2)
            even = lax.rem(local_id, 2) == 0
            block = back_ref[d * cap + j]
            turned = pltpu.roll(block, SUB // 2, 0)
            left = jnp.where(even, jnp.where(top, block, 0.0), jnp.where(top, 0.0, turned))
            right = jnp.where(even, jnp.where(top, turned, 0.0), jnp.where(top, 0.0, block))
            out_ref[group] = out_ref[group] + jnp.concatenate([left, right], axis=1)
            return inner

        return lax.fori_loop(0, ids_ref[d * LANES], row, carry)

    lax.fori_loop(0, peers, peer, 0)
    out_ref[...] = image_ref[...] * out_ref[...] / sensitivity_ref[...]


def local(image, sensitivity, system_blocks, tile_slab, tile_block, background):
    reps = lax.axis_size("rep")
    peers = lax.axis_size("slab") * reps
    tiles_here, _, width = system_blocks.shape
    planes, local_rows, columns = image.shape
    assert columns == 2 * LANES and width == SUB * LANES and local_rows % SUB == 0
    per_owner = local_rows * columns // width
    cap = CAP
    ids, slot = pl.pallas_call(
        functools.partial(
            route_kernel,
            peers=peers,
            reps=reps,
            per_plane=per_owner * reps,
            per_owner=per_owner,
            cap=cap,
        ),
        in_specs=[spec(SMEM), spec(SMEM)],
        out_specs=(spec(SMEM), spec(SMEM)),
        out_shape=(
            jax.ShapeDtypeStruct((peers * LANES,), jnp.int32),
            jax.ShapeDtypeStruct((tiles_here,), jnp.int32),
        ),
        name="route",
    )(tile_slab.reshape(-1), tile_block)

    def exchange(array):
        return lax.all_to_all(array, AXES, split_axis=0, concat_axis=0, tiled=True)

    asked = exchange(ids.reshape(peers, LANES)).reshape(-1)
    image_tiles = image.reshape(-1, SUB, columns)
    served = pl.pallas_call(
        functools.partial(serve_kernel, peers=peers, cap=cap),
        in_specs=[spec(SMEM), spec(VMEM)],
        out_specs=spec(VMEM),
        out_shape=jax.ShapeDtypeStruct((peers * cap, SUB, LANES), jnp.bfloat16),
        name="serve",
    )(asked, image_tiles)
    blocks = exchange(served.reshape(peers, cap, SUB, LANES)).reshape(served.shape)
    back = pl.pallas_call(
        project_kernel,
        in_specs=[spec(SMEM), spec(VMEM), spec(VMEM), spec(VMEM)],
        out_specs=spec(VMEM),
        out_shape=jax.ShapeDtypeStruct(served.shape, jnp.float32),
        name="project",
    )(slot, blocks, system_blocks, background)
    received = exchange(back.reshape(peers, cap, SUB, LANES)).reshape(back.shape)
    updated = pl.pallas_call(
        functools.partial(update_kernel, peers=peers, cap=cap),
        in_specs=[spec(SMEM), spec(VMEM), spec(VMEM), spec(VMEM)],
        out_specs=spec(VMEM),
        out_shape=jax.ShapeDtypeStruct(image_tiles.shape, jnp.float32),
        name="update",
    )(asked, received, image_tiles, sensitivity.reshape(image_tiles.shape))
    return updated.reshape(image.shape)


def solution(mesh):
    return jax.shard_map(
        local,
        mesh=mesh,
        in_specs=(
            P("slab", "rep", None),
            P("slab", "rep", None),
            P(("slab", "rep"), None, None),
            P(("slab", "rep"), None),
            P(("slab", "rep")),
            P(("slab", "rep"), None),
        ),
        out_specs=P("slab", "rep", None),
        check_vma=False,
    )
```

time: 105 us -> 72.9 us (0.69)
  waiting for transfers between devices: 26.1 us -> 0 us
  Pallas kernels: 0 us -> 16.1 us
  local copies, waits for them, and re-layouts: 10.5 us -> 0 us
  blocking collectives: 46.1 us -> 56.4 us
  starting transfers between devices: 9.38 us -> 0 us
  other arithmetic: 8.13 us -> 0 us
  matrix products: 4.17 us -> 0 us
    all_to_all x2 -> x0, waiting for transfers between devices: 26.1 us -> none  [the longest x1 19.9 us: local(): lax.all_to_all(lax.all_to_all(back_buffer, 'slab', split_axis=0, concat_a...]
    pallas_call x0 -> x4, Pallas kernels: none -> 16.1 us  [the longest x1 8.23 us: local(): pl.pallas_call(project_kernel, in_specs=[spec(SMEM), spec(VMEM), spec(VME...]
    all_to_all x4 -> x3, blocking collectives: 46.1 us -> 56.4 us  [exchange(): return lax.all_to_all(array, AXES, split_axis=0, concat_axis=0, tiled=True)]
    all_to_all x2 -> x0, starting transfers between devices: 9.38 us -> none  [the longest x1 5.83 us: local(): lax.all_to_all(lax.all_to_all(id_buffer, 'slab', split_axis=0, concat_axi...]
    dot_general x2 -> x0, matrix products: 4.17 us -> none  [the longest x1 3.52 us: local(): jnp.einsum('tev,tv->te', system_blocks, emission_cell_entries, preferred_...]
    all_to_all x7 -> x0, local copies, waits for them, and re-layouts: 3.2 us -> none  [the longest x1 1.39 us: local(): lax.all_to_all(back_buffer, 'slab', split_axis=0, concat_axis=0, tiled=True)]
    scatter x3 -> x0, local copies, waits for them, and re-layouts: 3.11 us -> none  [the longest x1 1.6 us: local(): back_buffer = jnp.zeros((slab_count, replica_total, CAP, width), jnp.floa...]
    scatter-add x1 -> x0, other arithmetic: 3 us -> none  [local(): owned = jnp.zeros(local_blocks.shape, jnp.float32).at[asked.reshape(-1)]....]
  transfers between devices with their start and end apart: 2 -> 0, of which waited for: 2 -> 0; matrix products, arithmetic and copies ran while one was open for 1% -> 0% of each run, Pallas kernels for 0% -> 0%
where the time goes in v1:
time: 72.9 us; the launch traced here: 72.5 us
  blocking collectives  56.4 us (77%)
  Pallas kernels  16.1 us (22%)
    all_to_all x3, blocking collectives, exchange(): return lax.all_to_all(array, AXES, split_axis=0, concat_axis=0, tiled=True)  56.4 us
    pallas_call x1, Pallas kernels, local(): pl.pallas_call(project_kernel, in_specs=[spec(SMEM), spec(VMEM), spec(VME...  8.23 us
    pallas_call x1, Pallas kernels, local(): pl.pallas_call(functools.partial(update_kernel, peers=peers, cap=cap), in...  3.65 us
    pallas_call x1, Pallas kernels, local(): pl.pallas_call(functools.partial(serve_kernel, peers=peers, cap=cap), in_...  2.56 us
    pallas_call x1, Pallas kernels, local(): pl.pallas_call(functools.partial(route_kernel, peers=peers, reps=reps, pe...  1.62 us

profile of v1, /device:TPU:0, one launch (start us, length us, event | category | flops | bytes accessed | tf_op | source)
XLA Modules:
  0.0 72.5 jit_solution(8300683204708513824)
XLA Ops:
  0.0 1.6 %route.1 = (s32[4096]{0:T(1024)}, s32[16]{0:T(128)}) custom-call(s32[16]{0:T(128)} %bitcast.20, s32[16]{0:T(128)} %block_ref.1), custom_call_target="tpu_custom_call" | custom-call | tf_op jit(solution)/shard_map/route/pallas_call | solution.py:109
  1.6 14.5 %all_to_all.19 = s32[32,1,128]{2,1,0:T(1,128)} all-to-all(s32[32,1,128]{2,1,0:T(1,128)} %bitcast.19), channel_id=1, replica_groups=mesh['slab'=4,'rep'=8] {'slab','rep'}, dimensions={0} | all-to-all | bytes 32768 | tf_op jit(solution)/shard_map/all_to_all | solution.py:128
  16.1 2.6 %serve.1 = bf16[192,8,128]{2,1,0:T(8,128)(2,1)} custom-call(s32[4096]{0:T(1024)} %bitcast.17, f32[144,8,256]{2,1,0:T(8,128)} %bitcast.10), custom_call_target="tpu_custom_call" | custom-call | tf_op jit(solution)/shard_map/serve/pallas_call | solution.py:132
  18.7 16.7 %all_to_all.20 = bf16[32,6,8,128]{3,2,1,0:T(8,128)(2,1)} all-to-all(bf16[32,6,8,128]{3,2,1,0:T(8,128)(2,1)} %bitcast.15), channel_id=1, replica_groups=mesh['slab'=4,'rep'=8] {'slab','rep'}, dimensions={0} | all-to-all | bytes 786432 | tf_op jit(solution)/shard_map/all_to_all | solution.py:128
  35.4 8.2 %project.1 = f32[192,8,128]{2,1,0:T(8,128)} custom-call(s32[16]{0:T(128)} %get-tuple-element.8.slot_ref, bf16[192,8,128]{2,1,0:T(8,128)(2,1)} %bitcast.14, bf16[16,128,1024]{2,1,0:T(8,128)(2,1)} %system_ref.1, bf16[16,128]{1,0:T(8,128)(2,1)} %background_ref.1), custom_call_target="tpu_custom_call" | custom-call | tf_op jit(solution)/shard_map/project/pallas_call | solution.py:140
  43.7 25.2 %all_to_all.21 = f32[32,6,8,128]{3,2,1,0:T(8,128)} all-to-all(f32[32,6,8,128]{3,2,1,0:T(8,128)} %bitcast.12), channel_id=1, replica_groups=mesh['slab'=4,'rep'=8] {'slab','rep'}, dimensions={0} | all-to-all | bytes 1572864 | tf_op jit(solution)/shard_map/all_to_all | solution.py:128
  68.8 3.7 %update.1 = f32[144,8,256]{2,1,0:T(8,128)} custom-call(s32[4096]{0:T(1024)} %bitcast.18, f32[192,8,128]{2,1,0:T(8,128)} %bitcast.13, f32[144,8,256]{2,1,0:T(8,128)} %bitcast.11, f32[144,8,256]{2,1,0:T(8,128)} %bitcast.16), custom_call_target="tpu_custom_call" | custom-call | tf_op jit(solution)/shard_map/update/pallas_call | solution.py:148

commit v2 on v1

--- a/solution.py
+++ b/solution.py
@@ -12,6 +12,9 @@
 AXES = ("slab", "rep")
 SMEM = pltpu.SMEM
 VMEM = pltpu.VMEM
+PARAMS = pltpu.CompilerParams(vmem_limit_bytes=8 << 20)
+CODE_TOP = 32000.0
+LEAST = 2.0**-100
 
 
 def spec(space):
@@ -22,7 +25,7 @@
     return lax.broadcasted_iota(jnp.int32, (SUB, LANES), 0) < SUB // 2
 
 
-def route_kernel(slab_ref, block_ref, ids_ref, slot_ref, *, peers, reps, per_plane, per_owner, cap):
+def route_kernel(slab_ref, block_ref, ids_ref, slot_ref, *, peers, reps, per_plane, per_owner):
     for d in range(peers):
         ids_ref[d * LANES] = 0
     for t in range(slot_ref.shape[0]):
@@ -33,7 +36,7 @@
         position = ids_ref[d * LANES]
         ids_ref[d * LANES] = position + 1
         ids_ref[d * LANES + 1 + position] = plane * per_owner + lax.rem(within, per_owner)
-        slot_ref[t] = d * cap + position
+        slot_ref[t] = d * SUB + position
 
 
 def serve_kernel(ids_ref, image_ref, out_ref, *, peers, cap):
@@ -55,12 +58,12 @@
     lax.fori_loop(0, peers, peer, 0)
 
 
-def project_kernel(slot_ref, blocks_ref, system_ref, background_ref, out_ref):
+def project_kernel(slot_ref, blocks_ref, system_ref, background_ref, out_ref, power_ref, *, peers, cap):
     half = SUB // 2
     order = [(k % 2) * half + k // 2 for k in range(SUB)]
     for t in range(system_ref.shape[0]):
-        slot = slot_ref[t]
-        block = blocks_ref[slot].astype(jnp.float32)
+        d, position = lax.div(slot_ref[t], SUB), lax.rem(slot_ref[t], SUB)
+        block = blocks_ref[d * cap + position].astype(jnp.float32)
         line = jnp.concatenate([block[j : j + 1] for j in order], axis=1).astype(jnp.bfloat16)
         system = system_ref[t]
         forward = lax.dot_general(
@@ -70,22 +73,34 @@
             jnp.bfloat16
         )
         back = jnp.dot(inverse, system, preferred_element_type=jnp.float32)
-        out_ref[slot] = jnp.concatenate(
+        largest = jnp.broadcast_to(jnp.max(back, axis=1, keepdims=True), (1, LANES))
+        power = jnp.ceil(jnp.log2(jnp.maximum(largest, LEAST)))
+        power_ref[d, pl.ds(position, 1)] = power.astype(jnp.int32)
+        tile = jnp.concatenate(
             [back[:, order.index(j) * LANES : (order.index(j) + 1) * LANES] for j in range(SUB)],
             axis=0,
         )
+        codes = tile * (CODE_TOP * jnp.exp2(-power)) + 0.5
+        out_ref[d * (cap + 1) + position] = codes.astype(jnp.int32).astype(jnp.int16)
+    for d in range(peers):
+        out_ref[d * (cap + 1) + cap] = power_ref[d].astype(jnp.int16)
 
 
 def update_kernel(ids_ref, back_ref, image_ref, sensitivity_ref, out_ref, *, peers, cap):
     top = half_rows()
+    sublane = lax.broadcasted_iota(jnp.int32, (SUB, LANES), 0)
     out_ref[...] = jnp.zeros(out_ref.shape, jnp.float32)
 
     def peer(d, carry):
+        powers = back_ref[d * (cap + 1) + cap].astype(jnp.int32)
+
         def row(j, inner):
             local_id = ids_ref[d * LANES + 1 + j]
             group = lax.div(local_id, 2)
             even = lax.rem(local_id, 2) == 0
-            block = back_ref[d * cap + j]
+            power = jnp.sum(jnp.where(sublane == j, powers, 0), axis=0, keepdims=True)
+            step = jnp.exp2(power.astype(jnp.float32)) * (1.0 / CODE_TOP)
+            block = back_ref[d * (cap + 1) + j].astype(jnp.int32).astype(jnp.float32) * step
             turned = pltpu.roll(block, SUB // 2, 0)
             left = jnp.where(even, jnp.where(top, block, 0.0), jnp.where(top, 0.0, turned))
             right = jnp.where(even, jnp.where(top, turned, 0.0), jnp.where(top, 0.0, block))
@@ -113,7 +128,6 @@
             reps=reps,
             per_plane=per_owner * reps,
             per_owner=per_owner,
-            cap=cap,
         ),
         in_specs=[spec(SMEM), spec(SMEM)],
         out_specs=(spec(SMEM), spec(SMEM)),
@@ -121,6 +135,7 @@
             jax.ShapeDtypeStruct((peers * LANES,), jnp.int32),
             jax.ShapeDtypeStruct((tiles_here,), jnp.int32),
         ),
+        compiler_params=PARAMS,
         name="route",
     )(tile_slab.reshape(-1), tile_block)
 
@@ -134,22 +149,26 @@
         in_specs=[spec(SMEM), spec(VMEM)],
         out_specs=spec(VMEM),
         out_shape=jax.ShapeDtypeStruct((peers * cap, SUB, LANES), jnp.bfloat16),
+        compiler_params=PARAMS,
         name="serve",
     )(asked, image_tiles)
     blocks = exchange(served.reshape(peers, cap, SUB, LANES)).reshape(served.shape)
     back = pl.pallas_call(
-        project_kernel,
+        functools.partial(project_kernel, peers=peers, cap=cap),
         in_specs=[spec(SMEM), spec(VMEM), spec(VMEM), spec(VMEM)],
         out_specs=spec(VMEM),
-        out_shape=jax.ShapeDtypeStruct(served.shape, jnp.float32),
+        out_shape=jax.ShapeDtypeStruct((peers * (cap + 1), SUB, LANES), jnp.int16),
+        scratch_shapes=[pltpu.VMEM((peers, SUB, LANES), jnp.int32)],
+        compiler_params=PARAMS,
         name="project",
     )(slot, blocks, system_blocks, background)
-    received = exchange(back.reshape(peers, cap, SUB, LANES)).reshape(back.shape)
+    received = exchange(back.reshape(peers, cap + 1, SUB, LANES)).reshape(back.shape)
     updated = pl.pallas_call(
         functools.partial(update_kernel, peers=peers, cap=cap),
         in_specs=[spec(SMEM), spec(VMEM), spec(VMEM), spec(VMEM)],
         out_specs=spec(VMEM),
         out_shape=jax.ShapeDtypeStruct(image_tiles.shape, jnp.float32),
+        compiler_params=PARAMS,
         name="update",
     )(asked, received, image_tiles, sensitivity.reshape(image_tiles.shape))
     return updated.reshape(image.shape)

time: 72.9 us -> 62.9 us (0.86)
  blocking collectives: 56.4 us -> 46.3 us
  Pallas kernels: 16.1 us -> 11.3 us
  local copies, waits for them, and re-layouts: 0 us -> 4.78 us
    all_to_all x3, blocking collectives: 56.4 us -> 46.3 us  [exchange(): return lax.all_to_all(array, AXES, split_axis=0, concat_axis=0, tiled=True)]
    unnamed x0 -> x14, local copies, waits for them, and re-layouts: none -> 4.78 us
    pallas_call x1, Pallas kernels: 8.23 us -> 5.73 us  [local(): pl.pallas_call(functools.partial(project_kernel, peers=peers, cap=cap), i...]
    pallas_call x1, Pallas kernels: 2.56 us -> 1.32 us  [local(): pl.pallas_call(functools.partial(serve_kernel, peers=peers, cap=cap), in_...]
    pallas_call x1, Pallas kernels: 3.65 us -> 2.7 us  [local(): pl.pallas_call(functools.partial(update_kernel, peers=peers, cap=cap), in...]
where the time goes in v2:
time: 62.9 us; the launch traced here: 62.4 us
  blocking collectives  46.3 us (74%)
  Pallas kernels  11.3 us (18%)
  local copies, waits for them, and re-layouts  4.78 us (8%)
    all_to_all x3, blocking collectives, exchange(): return lax.all_to_all(array, AXES, split_axis=0, concat_axis=0, tiled=True)  46.3 us
    pallas_call x1, Pallas kernels, local(): pl.pallas_call(functools.partial(project_kernel, peers=peers, cap=cap), i...  5.73 us
    unnamed x14, local copies, waits for them, and re-layouts  4.78 us
    pallas_call x1, Pallas kernels, local(): pl.pallas_call(functools.partial(update_kernel, peers=peers, cap=cap), in...  2.7 us
    pallas_call x1, Pallas kernels, local(): pl.pallas_call(functools.partial(route_kernel, peers=peers, reps=reps, pe...  1.57 us
    pallas_call x1, Pallas kernels, local(): pl.pallas_call(functools.partial(serve_kernel, peers=peers, cap=cap), in_...  1.32 us

profile of v2, /device:TPU:0, one launch (start us, length us, event | category | flops | bytes accessed | tf_op | source)
XLA Modules:
  0.0 62.4 jit_solution(11761867863884786306)
XLA Ops:
  0.0 0.0 copy-start.5
  0.0 0.7 %copy-done.5 = s32[16,1]{0,1:T(1,128)S(1)} copy-done((s32[16,1]{0,1:T(1,128)S(1)}, s32[16,1]{0,1:T(1,128)}, u32[]{:S(2)}) %copy-start.5) | copy-done | bytes 88
  0.7 0.0 copy-start.6
  0.7 0.7 %copy-done.6 = s32[16]{0:T(128)S(1)} copy-done((s32[16]{0:T(128)S(1)}, s32[16]{0:T(128)}, u32[]{:S(2)}) %copy-start.6) | copy-done | bytes 88
  1.3 1.6 %route.1 = (s32[4096]{0:T(1024)S(1)}, s32[16]{0:T(128)S(1)}) custom-call(s32[16]{0:T(128)S(1)} %bitcast.20, s32[16]{0:T(128)S(1)} %copy-done.6), custom_call_target="tpu_custom_call" | custom-call | tf_op jit(solution)/shard_map/route/pallas_call | solution.py:124
  2.9 14.3 %all_to_all.19 = s32[32,1,128]{2,1,0:T(1,128)S(1)} all-to-all(s32[32,1,128]{2,1,0:T(1,128)S(1)} %bitcast.19), channel_id=1, replica_groups=mesh['slab'=4,'rep'=8] {'slab','rep'}, dimensions={0} | all-to-all | bytes 32768 | tf_op jit(solution)/shard_map/all_to_all | solution.py:143
  17.2 0.0 copy-start
  17.2 1.3 %copy-done = f32[36,32,256]{2,1,0:T(8,128)S(1)} copy-done((f32[36,32,256]{2,1,0:T(8,128)S(1)}, f32[36,32,256]{2,1,0:T(8,128)}, u32[]{:S(2)}) %copy-start) | copy-done | bytes 1179672
  18.4 0.0 copy-start.4
  18.4 1.3 %serve.1 = bf16[192,8,128]{2,1,0:T(8,128)(2,1)S(1)} custom-call(s32[4096]{0:T(1024)S(1)} %bitcast.17, f32[144,8,256]{2,1,0:T(8,128)S(1)} %bitcast.10), custom_call_target="tpu_custom_call" | custom-call | tf_op jit(solution)/shard_map/serve/pallas_call | solution.py:147
  19.8 15.1 %all_to_all.20 = bf16[32,6,8,128]{3,2,1,0:T(8,128)(2,1)S(1)} all-to-all(bf16[32,6,8,128]{3,2,1,0:T(8,128)(2,1)S(1)} %bitcast.15), channel_id=1, replica_groups=mesh['slab'=4,'rep'=8] {'slab','rep'}, dimensions={0} | all-to-all | bytes 786432 | tf_op jit(solution)/shard_map/all_to_all | solution.py:143
  34.9 0.0 copy-done.4
  34.9 0.0 copy-start.2
  34.9 2.2 %copy-done.2 = bf16[16,128,1024]{2,1,0:T(8,128)(2,1)S(1)} copy-done((bf16[16,128,1024]{2,1,0:T(8,128)(2,1)S(1)}, bf16[16,128,1024]{2,1,0:T(8,128)(2,1)}, u32[]{:S(2)}) %copy-start.2) | copy-done | bytes 4194328
  37.1 0.0 copy-start.1
  37.1 0.0 copy-start.3
  37.1 5.7 %project.1 = s16[224,8,128]{2,1,0:T(8,128)(2,1)S(1)} custom-call(s32[16]{0:T(128)S(1)} %get-tuple-element.8.slot_ref, bf16[192,8,128]{2,1,0:T(8,128)(2,1)S(1)} %bitcast.14, bf16[16,128,1024]{2,1,0:T(8,128)(2,1)S(1)} %copy-done.2, bf16[16,128]{1,0:T(8,128)(2,1)S(1)} %copy-done.4), custom_call_target="tpu_custom_call" | custom-call | tf_op jit(solution)/shard_map/project/pallas_call | solution.py:156
  42.8 16.9 %all_to_all.21 = s16[32,7,8,128]{3,2,1,0:T(8,128)(2,1)S(1)} all-to-all(s16[32,7,8,128]{3,2,1,0:T(8,128)(2,1)S(1)} %bitcast.12), channel_id=1, replica_groups=mesh['slab'=4,'rep'=8] {'slab','rep'}, dimensions={0} | all-to-all | bytes 917504 | tf_op jit(solution)/shard_map/all_to_all | solution.py:143
  59.7 0.0 copy-done.1
  59.7 0.0 copy-done.3
  59.7 2.7 %update.1 = f32[144,8,256]{2,1,0:T(8,128)} custom-call(s32[4096]{0:T(1024)S(1)} %bitcast.18, s16[224,8,128]{2,1,0:T(8,128)(2,1)S(1)} %bitcast.13, f32[144,8,256]{2,1,0:T(8,128)S(1)} %bitcast.11, f32[144,8,256]{2,1,0:T(8,128)S(1)} %bitcast.16), custom_call_target="tpu_custom_call" | custom-call | tf_op jit(solution)/shard_map/update/pallas_call | solution.py:166
Async XLA Ops:
  0.0 0.7 %copy-start.5 = (s32[16,1]{0,1:T(1,128)S(1)}, s32[16,1]{0,1:T(1,128)}, u32[]{:S(2)}) copy-start(s32[16,1]{0,1:T(1,128)} %param.9) | copy-start | bytes 196
  0.7 0.7 %copy-start.6 = (s32[16]{0:T(128)S(1)}, s32[16]{0:T(128)}, u32[]{:S(2)}) copy-start(s32[16]{0:T(128)} %block_ref.1) | copy-start | bytes 196
  17.2 1.3 %copy-start = (f32[36,32,256]{2,1,0:T(8,128)S(1)}, f32[36,32,256]{2,1,0:T(8,128)}, u32[]{:S(2)}) copy-start(f32[36,32,256]{2,1,0:T(8,128)} %param.6) | copy-start | bytes 3538948
  18.4 16.5 %copy-start.4 = (bf16[16,128]{1,0:T(8,128)(2,1)S(1)}, bf16[16,128]{1,0:T(8,128)(2,1)}, u32[]{:S(2)}) copy-start(bf16[16,128]{1,0:T(8,128)(2,1)} %background_ref.1) | copy-start | bytes 12292
  34.9 2.2 %copy-start.2 = (bf16[16,128,1024]{2,1,0:T(8,128)(2,1)S(1)}, bf16[16,128,1024]{2,1,0:T(8,128)(2,1)}, u32[]{:S(2)}) copy-start(bf16[16,128,1024]{2,1,0:T(8,128)(2,1)} %system_ref.1) | copy-start | bytes 12582916
  37.1 22.6 %copy-start.1 = (f32[36,32,256]{2,1,0:T(8,128)S(1)}, f32[36,32,256]{2,1,0:T(8,128)}, u32[]{:S(2)}) copy-start(f32[36,32,256]{2,1,0:T(8,128)} %param.6) | copy-start | bytes 3538948
  37.1 22.6 %copy-start.3 = (f32[36,32,256]{2,1,0:T(8,128)S(1)}, f32[36,32,256]{2,1,0:T(8,128)}, u32[]{:S(2)}) copy-start(f32[36,32,256]{2,1,0:T(8,128)} %param.7) | copy-start | bytes 3538948

commit v3 on v2

v3 whole, which is shorter than its diff:
```python
import functools
import jax
import jax.numpy as jnp
from jax import lax
from jax.experimental import pallas as pl
from jax.experimental.pallas import tpu as pltpu
from jax.sharding import PartitionSpec as P

CAP = 6
LANES = 128
SUB = 8
AXES = ("slab", "rep")
SMEM = pltpu.SMEM
VMEM = pltpu.VMEM
PARAMS = pltpu.CompilerParams(vmem_limit_bytes=8 << 20)
CODE_TOP = 32000.0
LEAST = 2.0**-100
WIDE = pltpu.CompilerParams(vmem_limit_bytes=52 << 20)


def spec(space):
    return pl.BlockSpec(memory_space=space)


def half_rows():
    return lax.broadcasted_iota(jnp.int32, (SUB, LANES), 0) < SUB // 2


def route_kernel(
    slab_in, block_in, ids_ref, slot_ref, slab_ref, block_ref, sems, *, peers, reps, per_plane, per_owner
):
    copies = (
        pltpu.make_async_copy(slab_in, slab_ref, sems.at[0]),
        pltpu.make_async_copy(block_in, block_ref, sems.at[1]),
    )
    for copy in copies:
        copy.start()
    for d in range(peers):
        ids_ref[d * LANES] = 0
    for copy in copies:
        copy.wait()
    for t in range(slot_ref.shape[0]):
        block = block_ref[t]
        plane = lax.div(block, per_plane)
        within = lax.rem(block, per_plane)
        d = slab_ref[t] * reps + lax.div(within, per_owner)
        position = ids_ref[d * LANES]
        ids_ref[d * LANES] = position + 1
        ids_ref[d * LANES + 1 + position] = plane * per_owner + lax.rem(within, per_owner)
        slot_ref[t] = d * SUB + position


def serve_kernel(ids_ref, image_ref, out_ref, list_ref, *, peers, cap):
    top = half_rows()

    def peer(d, carry):
        def row(j, inner):
            local_id = ids_ref[d * LANES + 1 + j]
            list_ref[1 + 2 * inner] = d * SUB + j
            list_ref[2 + 2 * inner] = local_id
            tile = image_ref[lax.div(local_id, 2)]
            left, right = tile[:, :LANES], tile[:, LANES:]
            even = jnp.where(top, left, pltpu.roll(right, SUB // 2, 0))
            odd = jnp.where(top, pltpu.roll(left, SUB // 2, 0), right)
            picked = jnp.where(lax.rem(local_id, 2) == 0, even, odd)
            out_ref[d * cap + j] = picked.astype(jnp.bfloat16)
            return inner + 1

        return lax.fori_loop(0, ids_ref[d * LANES], row, carry)

    list_ref[0] = lax.fori_loop(0, peers, peer, 0)


def project_kernel(
    slot_ref, blocks_ref, system_in, background_ref, out_ref, line_ref, power_ref, system_ref, sems,
    *, peers, cap
):
    half = SUB // 2
    tiles, tile_rows, width = system_ref.shape
    copies = [
        pltpu.make_async_copy(system_in.at[t], system_ref.at[t], sems.at[t]) for t in range(tiles)
    ]
    for copy in copies:
        copy.start()
    order = [(k % 2) * half + k // 2 for k in range(SUB)]
    places = [(lax.div(slot_ref[t], SUB), lax.rem(slot_ref[t], SUB)) for t in range(tiles)]
    for t, (d, position) in enumerate(places):
        block = blocks_ref[d * cap + position].astype(jnp.float32)
        for k, j in enumerate(order):
            line_ref[t : t + 1, k * LANES : (k + 1) * LANES] = block[j : j + 1]
    lines = line_ref[...].astype(jnp.bfloat16)
    row = lax.broadcasted_iota(jnp.int32, (tiles, tile_rows), 0)
    forward = jnp.zeros((tiles, tile_rows), jnp.float32)
    for t in range(tiles):
        copies[t].wait()
        every = lax.dot_general(
            lines, system_ref[t], (((1,), (1,)), ((), ())), preferred_element_type=jnp.float32
        )
        forward = jnp.where(row == t, every, forward)
    inverse = (1.0 / (forward + background_ref[...].astype(jnp.float32))).astype(jnp.bfloat16)
    for t in range(tiles):
        every = jnp.dot(inverse, system_ref[t], preferred_element_type=jnp.float32)
        line_ref[t : t + 1, :] = every[t : t + 1, :]
    back = line_ref[...]
    largest = jnp.broadcast_to(jnp.max(back, axis=1, keepdims=True), (tiles, LANES))
    power = jnp.ceil(jnp.log2(jnp.maximum(largest, LEAST)))
    scale = CODE_TOP * jnp.exp2(-power)
    power = power.astype(jnp.int32)
    codes = [
        (back[:, k * LANES : (k + 1) * LANES] * scale + 0.5).astype(jnp.int32) for k in range(SUB)
    ]
    for t, (d, position) in enumerate(places):
        power_ref[d, pl.ds(position, 1)] = power[t : t + 1]
        tile = jnp.concatenate([codes[order.index(j)][t : t + 1] for j in range(SUB)], axis=0)
        out_ref[d * (cap + 1) + position] = tile.astype(jnp.int16)
    for d in range(peers):
        out_ref[d * (cap + 1) + cap] = power_ref[d].astype(jnp.int16)


def update_kernel(
    list_ref, back_ref, image_ref, sensitivity_ref, out_ref, step_ref, *, peers, cap
):
    top = half_rows()
    out_ref[...] = jnp.zeros(out_ref.shape, jnp.float32)
    for d in range(peers):
        powers = back_ref[d * (cap + 1) + cap].astype(jnp.int32).astype(jnp.float32)
        step_ref[d] = jnp.exp2(powers) * (1.0 / CODE_TOP)

    def request(i, carry):
        place = list_ref[1 + 2 * i]
        local_id = list_ref[2 + 2 * i]
        d, j = lax.div(place, SUB), lax.rem(place, SUB)
        group = lax.div(local_id, 2)
        even = lax.rem(local_id, 2) == 0
        step = step_ref[d, pl.ds(j, 1)]
        block = back_ref[d * (cap + 1) + j].astype(jnp.int32).astype(jnp.float32) * step
        turned = pltpu.roll(block, SUB // 2, 0)
        left = jnp.where(even, jnp.where(top, block, 0.0), jnp.where(top, 0.0, turned))
        right = jnp.where(even, jnp.where(top, turned, 0.0), jnp.where(top, 0.0, block))
        out_ref[group] = out_ref[group] + jnp.concatenate([left, right], axis=1)
        return carry

    lax.fori_loop(0, list_ref[0], request, 0)
    out_ref[...] = image_ref[...] * out_ref[...] / sensitivity_ref[...]


def local(image, sensitivity, system_blocks, tile_slab, tile_block, background):
    reps = lax.axis_size("rep")
    peers = lax.axis_size("slab") * reps
    tiles_here, _, width = system_blocks.shape
    planes, local_rows, columns = image.shape
    assert columns == 2 * LANES and width == SUB * LANES and local_rows % SUB == 0
    per_owner = local_rows * columns // width
    cap = CAP
    ids, slot = pl.pallas_call(
        functools.partial(
            route_kernel,
            peers=peers,
            reps=reps,
            per_plane=per_owner * reps,
            per_owner=per_owner,
        ),
        in_specs=[spec(pltpu.HBM), spec(pltpu.HBM)],
        out_specs=(spec(SMEM), spec(SMEM)),
        scratch_shapes=[
            pltpu.SMEM((tiles_here,), jnp.int32),
            pltpu.SMEM((tiles_here,), jnp.int32),
            pltpu.SemaphoreType.DMA((2,)),
        ],
        out_shape=(
            jax.ShapeDtypeStruct((peers * LANES,), jnp.int32),
            jax.ShapeDtypeStruct((tiles_here,), jnp.int32),
        ),
        name="route",
    )(tile_slab.reshape(-1), tile_block)

    def exchange(array):
        return lax.all_to_all(array, AXES, split_axis=0, concat_axis=0, tiled=True)

    asked = exchange(ids.reshape(peers, LANES)).reshape(-1)
    image_tiles = image.reshape(-1, SUB, columns)
    served, requests = pl.pallas_call(
        functools.partial(serve_kernel, peers=peers, cap=cap),
        in_specs=[spec(SMEM), spec(VMEM)],
        out_specs=(spec(VMEM), spec(SMEM)),
        out_shape=(
            jax.ShapeDtypeStruct((peers * cap, SUB, LANES), jnp.bfloat16),
            jax.ShapeDtypeStruct((1 + 2 * peers * cap,), jnp.int32),
        ),
        compiler_params=PARAMS,
        name="serve",
    )(asked, image_tiles)
    blocks = exchange(served.reshape(peers, cap, SUB, LANES)).reshape(served.shape)
    back = pl.pallas_call(
        functools.partial(project_kernel, peers=peers, cap=cap),
        in_specs=[spec(SMEM), spec(VMEM), spec(pltpu.HBM), spec(VMEM)],
        out_specs=spec(VMEM),
        out_shape=jax.ShapeDtypeStruct((peers * (cap + 1), SUB, LANES), jnp.int16),
        scratch_shapes=[
            pltpu.VMEM((tiles_here, width), jnp.float32),
            pltpu.VMEM((peers, SUB, LANES), jnp.int32),
            pltpu.VMEM(system_blocks.shape, jnp.bfloat16),
            pltpu.SemaphoreType.DMA((tiles_here,)),
        ],
        compiler_params=WIDE,
        name="project",
    )(slot, blocks, system_blocks, background)
    received = exchange(back.reshape(peers, cap + 1, SUB, LANES)).reshape(back.shape)
    updated = pl.pallas_call(
        functools.partial(update_kernel, peers=peers, cap=cap),
        in_specs=[spec(SMEM), spec(VMEM), spec(VMEM), spec(VMEM)],
        out_specs=spec(VMEM),
        out_shape=jax.ShapeDtypeStruct(image_tiles.shape, jnp.float32),
        scratch_shapes=[pltpu.VMEM((peers, SUB, LANES), jnp.float32)],
        compiler_params=PARAMS,
        name="update",
    )(requests, received, image_tiles, sensitivity.reshape(image_tiles.shape))
    return updated.reshape(image.shape)


def solution(mesh):
    return jax.shard_map(
        local,
        mesh=mesh,
        in_specs=(
            P("slab", "rep", None),
            P("slab", "rep", None),
            P(("slab", "rep"), None, None),
            P(("slab", "rep"), None),
            P(("slab", "rep")),
            P(("slab", "rep"), None),
        ),
        out_specs=P("slab", "rep", None),
        check_vma=False,
    )
```

time: 62.9 us -> 60.6 us (0.963)
  local copies, waits for them, and re-layouts: 4.78 us -> 1.29 us
  Pallas kernels: 11.3 us -> 12.8 us
    unnamed x14 -> x10, local copies, waits for them, and re-layouts: 4.78 us -> 1.29 us
    pallas_call x1, Pallas kernels: 5.73 us -> 6.63 us  [local(): pl.pallas_call(functools.partial(project_kernel, peers=peers, cap=cap), i...]
    pallas_call x1, Pallas kernels: 1.32 us -> 2.12 us  [local(): pl.pallas_call(functools.partial(serve_kernel, peers=peers, cap=cap), in_...]
where the time goes in v3:
time: 60.6 us
  blocking collectives  46.5 us (77%)
  Pallas kernels  12.8 us (21%)
  local copies, waits for them, and re-layouts  1.29 us (2%)
    all_to_all x3, blocking collectives, exchange(): return lax.all_to_all(array, AXES, split_axis=0, concat_axis=0, tiled=True)  46.5 us
    pallas_call x1, Pallas kernels, local(): pl.pallas_call(functools.partial(project_kernel, peers=peers, cap=cap), i...  6.63 us
    pallas_call x1, Pallas kernels, local(): pl.pallas_call(functools.partial(update_kernel, peers=peers, cap=cap), in...  2.31 us
    pallas_call x1, Pallas kernels, local(): pl.pallas_call(functools.partial(serve_kernel, peers=peers, cap=cap), in_...  2.12 us
    pallas_call x1, Pallas kernels, local(): pl.pallas_call(functools.partial(route_kernel, peers=peers, reps=reps, pe...  1.77 us
    unnamed x10, local copies, waits for them, and re-layouts  1.29 us

profile of v3, /device:TPU:0, one launch (start us, length us, event | category | flops | bytes accessed | tf_op | source)
XLA Modules:
  0.0 60.6 jit_solution(13334778085442209553)
XLA Ops:
  0.0 0.0 copy-start.3
  0.0 1.8 %route.1 = (s32[4096]{0:T(1024)}, s32[16]{0:T(128)}) custom-call(s32[16]{0:T(128)} %bitcast.19, s32[16]{0:T(128)} %block_in.1), custom_call_target="tpu_custom_call" | custom-call | tf_op jit(solution)/shard_map/route/pallas_call | solution.py:155
  1.8 0.0 copy-start.4
  1.8 14.4 %all_to_all.19 = s32[32,1,128]{2,1,0:T(1,128)S(1)} all-to-all(s32[32,1,128]{2,1,0:T(1,128)} %bitcast.18), channel_id=1, replica_groups=mesh['slab'=4,'rep'=8] {'slab','rep'}, dimensions={0} | all-to-all | bytes 32768 | tf_op jit(solution)/shard_map/all_to_all | solution.py:178
  16.2 0.0 copy-start
  16.2 1.3 %copy-done = f32[36,32,256]{2,1,0:T(8,128)S(1)} copy-done((f32[36,32,256]{2,1,0:T(8,128)S(1)}, f32[36,32,256]{2,1,0:T(8,128)}, u32[]{:S(2)}) %copy-start) | copy-done | bytes 1179672
  17.5 2.1 %serve.1 = (bf16[192,8,128]{2,1,0:T(8,128)(2,1)S(1)}, s32[385]{0:T(512)S(1)}) custom-call(s32[4096]{0:T(1024)S(1)} %bitcast.17, f32[144,8,256]{2,1,0:T(8,128)S(1)} %bitcast.10), custom_call_target="tpu_custom_call" | custom-call | tf_op jit(solution)/shard_map/serve/pallas_call | solution.py:182
  19.6 15.1 %all_to_all.20 = bf16[32,6,8,128]{3,2,1,0:T(8,128)(2,1)S(1)} all-to-all(bf16[32,6,8,128]{3,2,1,0:T(8,128)(2,1)S(1)} %bitcast.16), channel_id=1, replica_groups=mesh['slab'=4,'rep'=8] {'slab','rep'}, dimensions={0} | all-to-all | bytes 786432 | tf_op jit(solution)/shard_map/all_to_all | solution.py:178
  34.7 0.0 copy-done.3
  34.7 0.0 copy-done.4
  34.7 0.0 copy-start.1
  34.7 0.0 copy-start.2
  34.8 6.6 %project.1 = s16[224,8,128]{2,1,0:T(8,128)(2,1)S(1)} custom-call(s32[16]{0:T(128)S(1)} %copy-done.4, bf16[192,8,128]{2,1,0:T(8,128)(2,1)S(1)} %bitcast.14, bf16[16,128,1024]{2,1,0:T(8,128)(2,1)} %system_in.1, bf16[16,128]{1,0:T(8,128)(2,1)S(1)} %copy-done.3), custom_call_target="tpu_custom_call" | custom-call | tf_op jit(solution)/shard_map/project/pallas_call | solution.py:194
  41.4 16.9 %all_to_all.21 = s16[32,7,8,128]{3,2,1,0:T(8,128)(2,1)S(1)} all-to-all(s16[32,7,8,128]{3,2,1,0:T(8,128)(2,1)S(1)} %bitcast.13), channel_id=1, replica_groups=mesh['slab'=4,'rep'=8] {'slab','rep'}, dimensions={0} | all-to-all | bytes 917504 | tf_op jit(solution)/shard_map/all_to_all | solution.py:178
  58.3 0.0 copy-done.1
  58.3 0.0 copy-done.2
  58.3 2.3 %update.1 = f32[144,8,256]{2,1,0:T(8,128)} custom-call(s32[385]{0:T(512)S(1)} %get-tuple-element.10.list_ref, s16[224,8,128]{2,1,0:T(8,128)(2,1)S(1)} %bitcast.12, f32[144,8,256]{2,1,0:T(8,128)S(1)} %bitcast.11, f32[144,8,256]{2,1,0:T(8,128)S(1)} %bitcast.15), custom_call_target="tpu_custom_call" | custom-call | tf_op jit(solution)/shard_map/update/pallas_call | solution.py:209
Async XLA Ops:
  0.0 34.7 %copy-start.3 = (bf16[16,128]{1,0:T(8,128)(2,1)S(1)}, bf16[16,128]{1,0:T(8,128)(2,1)}, u32[]{:S(2)}) copy-start(bf16[16,128]{1,0:T(8,128)(2,1)} %background_ref.1) | copy-start | bytes 12292
  1.8 33.0 %copy-start.4 = (s32[16]{0:T(128)S(1)}, s32[16]{0:T(128)}, u32[]{:S(2)}) copy-start(s32[16]{0:T(128)} %get-tuple-element.11.slot_ref) | copy-start | bytes 196
  16.2 1.3 %copy-start = (f32[36,32,256]{2,1,0:T(8,128)S(1)}, f32[36,32,256]{2,1,0:T(8,128)}, u32[]{:S(2)}) copy-start(f32[36,32,256]{2,1,0:T(8,128)} %param.6) | copy-start | bytes 3538948
  34.7 23.5 %copy-start.1 = (f32[36,32,256]{2,1,0:T(8,128)S(1)}, f32[36,32,256]{2,1,0:T(8,128)}, u32[]{:S(2)}) copy-start(f32[36,32,256]{2,1,0:T(8,128)} %param.6) | copy-start | bytes 3538948
  34.7 23.5 %copy-start.2 = (f32[36,32,256]{2,1,0:T(8,128)S(1)}, f32[36,32,256]{2,1,0:T(8,128)}, u32[]{:S(2)}) copy-start(f32[36,32,256]{2,1,0:T(8,128)} %param.7) | copy-start | bytes 3538948

commit v4 on v3

--- a/solution.py
+++ b/solution.py
@@ -88,16 +88,14 @@
         block = blocks_ref[d * cap + position].astype(jnp.float32)
         for k, j in enumerate(order):
             line_ref[t : t + 1, k * LANES : (k + 1) * LANES] = block[j : j + 1]
-    lines = line_ref[...].astype(jnp.bfloat16)
-    row = lax.broadcasted_iota(jnp.int32, (tiles, tile_rows), 0)
-    forward = jnp.zeros((tiles, tile_rows), jnp.float32)
+    lines = line_ref[...].T.astype(jnp.bfloat16)
+    column = lax.broadcasted_iota(jnp.int32, (tile_rows, tiles), 1)
+    forward = jnp.zeros((tile_rows, tiles), jnp.float32)
     for t in range(tiles):
         copies[t].wait()
-        every = lax.dot_general(
-            lines, system_ref[t], (((1,), (1,)), ((), ())), preferred_element_type=jnp.float32
-        )
-        forward = jnp.where(row == t, every, forward)
-    inverse = (1.0 / (forward + background_ref[...].astype(jnp.float32))).astype(jnp.bfloat16)
+        every = jnp.dot(system_ref[t], lines, preferred_element_type=jnp.float32)
+        forward = jnp.where(column == t, every, forward)
+    inverse = (1.0 / (forward.T + background_ref[...].astype(jnp.float32))).astype(jnp.bfloat16)
     for t in range(tiles):
         every = jnp.dot(inverse, system_ref[t], preferred_element_type=jnp.float32)
         line_ref[t : t + 1, :] = every[t : t + 1, :]

time: 60.6 us -> 60 us (0.990)
  Pallas kernels: 12.8 us -> 12 us
where the time goes in v4:
time: 60 us; the launch traced here: 59.8 us
  blocking collectives  46.5 us (78%)
  Pallas kernels  12 us (20%)
  local copies, waits for them, and re-layouts  1.29 us (2%)
    all_to_all x3, blocking collectives, exchange(): return lax.all_to_all(array, AXES, split_axis=0, concat_axis=0, tiled=True)  46.5 us
    pallas_call x1, Pallas kernels, local(): pl.pallas_call(functools.partial(project_kernel, peers=peers, cap=cap), i...  6.06 us
    pallas_call x1, Pallas kernels, local(): pl.pallas_call(functools.partial(update_kernel, peers=peers, cap=cap), in...  2.15 us
    pallas_call x1, Pallas kernels, local(): pl.pallas_call(functools.partial(serve_kernel, peers=peers, cap=cap), in_...  2.02 us
    pallas_call x1, Pallas kernels, local(): pl.pallas_call(functools.partial(route_kernel, peers=peers, reps=reps, pe...  1.77 us
    unnamed x10, local copies, waits for them, and re-layouts  1.29 us

profile of v4, /device:TPU:0, one launch (start us, length us, event | category | flops | bytes accessed | tf_op | source)
XLA Modules:
  0.0 59.8 jit_solution(16652338104064417056)
XLA Ops:
  0.0 0.0 copy-start.3
  0.0 1.8 %route.1 = (s32[4096]{0:T(1024)}, s32[16]{0:T(128)}) custom-call(s32[16]{0:T(128)} %bitcast.19, s32[16]{0:T(128)} %block_in.1), custom_call_target="tpu_custom_call" | custom-call | tf_op jit(solution)/shard_map/route/pallas_call | solution.py:153
  1.8 0.0 copy-start.4
  1.8 14.4 %all_to_all.19 = s32[32,1,128]{2,1,0:T(1,128)S(1)} all-to-all(s32[32,1,128]{2,1,0:T(1,128)} %bitcast.18), channel_id=1, replica_groups=mesh['slab'=4,'rep'=8] {'slab','rep'}, dimensions={0} | all-to-all | bytes 32768 | tf_op jit(solution)/shard_map/all_to_all | solution.py:176
  16.2 0.0 copy-start
  16.2 1.3 %copy-done = f32[36,32,256]{2,1,0:T(8,128)S(1)} copy-done((f32[36,32,256]{2,1,0:T(8,128)S(1)}, f32[36,32,256]{2,1,0:T(8,128)}, u32[]{:S(2)}) %copy-start) | copy-done | bytes 1179672
  17.5 2.0 %serve.1 = (bf16[192,8,128]{2,1,0:T(8,128)(2,1)S(1)}, s32[385]{0:T(512)S(1)}) custom-call(s32[4096]{0:T(1024)S(1)} %bitcast.17, f32[144,8,256]{2,1,0:T(8,128)S(1)} %bitcast.10), custom_call_target="tpu_custom_call" | custom-call | tf_op jit(solution)/shard_map/serve/pallas_call | solution.py:180
  19.5 15.1 %all_to_all.20 = bf16[32,6,8,128]{3,2,1,0:T(8,128)(2,1)S(1)} all-to-all(bf16[32,6,8,128]{3,2,1,0:T(8,128)(2,1)S(1)} %bitcast.16), channel_id=1, replica_groups=mesh['slab'=4,'rep'=8] {'slab','rep'}, dimensions={0} | all-to-all | bytes 786432 | tf_op jit(solution)/shard_map/all_to_all | solution.py:176
  34.6 0.0 copy-done.3
  34.6 0.0 copy-done.4
  34.6 0.0 copy-start.1
  34.6 0.0 copy-start.2
  34.7 6.1 %project.1 = s16[224,8,128]{2,1,0:T(8,128)(2,1)S(1)} custom-call(s32[16]{0:T(128)S(1)} %copy-done.4, bf16[192,8,128]{2,1,0:T(8,128)(2,1)S(1)} %bitcast.14, bf16[16,128,1024]{2,1,0:T(8,128)(2,1)} %system_in.1, bf16[16,128]{1,0:T(8,128)(2,1)S(1)} %copy-done.3), custom_call_target="tpu_custom_call" | custom-call | tf_op jit(solution)/shard_map/project/pallas_call | solution.py:192
  40.7 16.9 %all_to_all.21 = s16[32,7,8,128]{3,2,1,0:T(8,128)(2,1)S(1)} all-to-all(s16[32,7,8,128]{3,2,1,0:T(8,128)(2,1)S(1)} %bitcast.13), channel_id=1, replica_groups=mesh['slab'=4,'rep'=8] {'slab','rep'}, dimensions={0} | all-to-all | bytes 917504 | tf_op jit(solution)/shard_map/all_to_all | solution.py:176
  57.6 0.0 copy-done.1
  57.6 0.0 copy-done.2
  57.6 2.2 %update.1 = f32[144,8,256]{2,1,0:T(8,128)} custom-call(s32[385]{0:T(512)S(1)} %get-tuple-element.10.list_ref, s16[224,8,128]{2,1,0:T(8,128)(2,1)S(1)} %bitcast.12, f32[144,8,256]{2,1,0:T(8,128)S(1)} %bitcast.11, f32[144,8,256]{2,1,0:T(8,128)S(1)} %bitcast.15), custom_call_target="tpu_custom_call" | custom-call | tf_op jit(solution)/shard_map/update/pallas_call | solution.py:207
Async XLA Ops:
  0.0 34.6 %copy-start.3 = (bf16[16,128]{1,0:T(8,128)(2,1)S(1)}, bf16[16,128]{1,0:T(8,128)(2,1)}, u32[]{:S(2)}) copy-start(bf16[16,128]{1,0:T(8,128)(2,1)} %background_ref.1) | copy-start | bytes 12292
  1.8 32.9 %copy-start.4 = (s32[16]{0:T(128)S(1)}, s32[16]{0:T(128)}, u32[]{:S(2)}) copy-start(s32[16]{0:T(128)} %get-tuple-element.11.slot_ref) | copy-start | bytes 196
  16.2 1.3 %copy-start = (f32[36,32,256]{2,1,0:T(8,128)S(1)}, f32[36,32,256]{2,1,0:T(8,128)}, u32[]{:S(2)}) copy-start(f32[36,32,256]{2,1,0:T(8,128)} %param.6) | copy-start | bytes 3538948
  34.6 23.0 %copy-start.1 = (f32[36,32,256]{2,1,0:T(8,128)S(1)}, f32[36,32,256]{2,1,0:T(8,128)}, u32[]{:S(2)}) copy-start(f32[36,32,256]{2,1,0:T(8,128)} %param.6) | copy-start | bytes 3538948
  34.6 23.0 %copy-start.2 = (f32[36,32,256]{2,1,0:T(8,128)S(1)}, f32[36,32,256]{2,1,0:T(8,128)}, u32[]{:S(2)}) copy-start(f32[36,32,256]{2,1,0:T(8,128)} %param.7) | copy-start | bytes 3538948
